TPU v7x, 1024 devices: a whole 4x8x16 slice. The times are simulated.
1024 devices in a mesh: vb: 32 (over x, z_lo), vc: 32 (over z_hi, y, core).
Axes of the slice: x: 4, y: 8, z: 16 (z_hi: 2, z_lo: 8; z = z_hi * 8 + z_lo), core: 2. Of those that a mesh axis runs over, the one named last changes fastest.
Arguments:
- integrals: float32 [2, 512, 512, 512], P(None, 'vb', 'vc'), may hold values from -0.25 to 0.25
- doubles: float32 [3, 512, 512], P(None, 'vb'), may hold values from -6 to 6
- eps_occ: float32 [100], replicated, may hold values from -2 to -0.5
- eps_virt: float32 [512], replicated, may hold values from 0.2 to 3
- triple: int32 [3], replicated, may hold values from 0 to 99
- energy_order: int32 [512], replicated, may hold values from 0 to 511, each once
Outputs:
- amplitudes: float32 [512, 512, 512], P('vb', 'vc')
- grad: float32 [512, 512], P('vb', 'vc')
Inputs may be any that keep to these rules, and one draw needn't show every extreme that they name: `energy_order`: each of 0 to 511 appears once.
All inputs are finite; a program needn't handle non-finite values.
Results may differ from a plain program's by a relative error of at most 0.00007.
Values sent between devices are 32-bit elements; how exact they have to be, the bound alone decides.
A program may use at most 64 MiB of HBM per device.

v0:
```python
import jax
import jax.numpy as jnp
from jax import lax
from jax.sharding import Mesh
from jax.sharding import PartitionSpec as P

V = 512
NOCC = 100
VB = ("vb_0", "vb_1")


def gather_axes(shard, axes, dim):
    if not axes:
        return shard
    nearer = lax.all_gather(shard, axes[-1], axis=dim, tiled=True)
    return gather_axes(nearer, axes[:-1], dim)


def in_blocks(shard, dim, size):
    before, after = (shard.shape[:dim], shard.shape[dim + 1 :])
    return jnp.moveaxis(shard.reshape(*before, size, -1, *after), dim, 0)


def summed_on_arrival(shard, axis, dim):
    pieces = in_blocks(shard, dim, lax.axis_size(axis))
    arrived = lax.all_to_all(pieces, axis, split_axis=0, concat_axis=0, tiled=True)
    return arrived.sum(axis=0)


def on_device(integrals, doubles, eps_occ, eps_virt, triple, energy_order):
    highest = lax.Precision.HIGHEST
    all_doubles = gather_axes(doubles, VB, 1)
    k_block = integrals[0]
    i_block = integrals[1]
    b_rows = k_block.shape[0]
    c_rows = k_block.shape[1]
    first_term = jnp.einsum("pqd,ad->pqa", k_block, all_doubles[0], precision=highest)
    second_local = jnp.einsum("pqd,bd->bqp", k_block, all_doubles[1], precision=highest)
    second_term = lax.all_to_all(second_local, VB, split_axis=0, concat_axis=2, tiled=True)
    third_local = jnp.einsum("pqd,cd->pcq", i_block, all_doubles[2], precision=highest)
    third_term = lax.all_to_all(third_local, "vc", split_axis=1, concat_axis=2, tiled=True)
    positions = jnp.arange(V, dtype=jnp.int32)
    one_hot = energy_order[:, None] == positions[None, :]
    virt_energy = jnp.sum(jnp.where(one_hot, eps_virt[None, :], jnp.float32(0.0)), axis=1)
    occ_positions = jnp.arange(NOCC, dtype=jnp.int32)
    occ_hot = triple[:, None] == occ_positions[None, :]
    occ_energy = jnp.sum(jnp.where(occ_hot, eps_occ[None, :], jnp.float32(0.0)))
    b_index = lax.axis_index(VB)
    c_index = lax.axis_index("vc")
    b_energy = lax.dynamic_slice_in_dim(virt_energy, b_index * b_rows, b_rows)
    c_energy = lax.dynamic_slice_in_dim(virt_energy, c_index * c_rows, c_rows)
    denominator = (
        occ_energy - b_energy[:, None, None] - c_energy[None, :, None] - virt_energy[None, None, :]
    )
    amplitudes = (first_term + second_term + third_term) / denominator
    grad_partial = jnp.einsum("bca,bcd->ad", amplitudes, k_block, precision=highest)
    row_sums = summed_on_arrival(grad_partial, VB, 0)
    grad = summed_on_arrival(row_sums, "vc", 1)
    return (amplitudes, grad)


def solution(mesh):
    split = Mesh(mesh.devices.reshape(4, 8, mesh.shape["vc"]), ("vb_0", "vb_1", "vc"))
    return jax.shard_map(
        on_device,
        mesh=split,
        in_specs=(P(None, VB, "vc", None), P(None, VB, None), P(), P(), P(), P()),
        out_specs=(P(VB, "vc", None), P(VB, "vc")),
        check_vma=False,
    )
```

profile of v0, /device:TPU:1, one launch (start us, length us, event | category | flops | bytes accessed | tf_op | source)
XLA Modules:
  0.0 334.1 jit_solution(5073025040260055075)
XLA Ops:
  7.2 53.0 %all_gather.6 = f32[3,128,512]{2,1,0:T(8,128)} all-gather(f32[3,16,512]{2,1,0:T(8,128)} %param.7), channel_id=1, replica_groups=mesh['vb_0'=4,'vb_1'=8,'vc'=32] {'vb_1'}, dimensions={1}, use_global_device_ids=true | all-gather | bytes 884736 | tf_op jit(solution)/shard_map/all_gather | solution.py:15
  60.2 56.6 %all-gather.2.cloned.1.call-done = f32[3,512,512]{2,1,0:T(8,128)} async-done(((f32[3,128,512]{2,1,0:T(8,128)}), f32[3,512,512]{2,1,0:T(8,128)}) %all-gather.2.cloned.1.call-update) | async-done | bytes 3145744 | tf_op jit(solution)/shard_map/all_gather | solution.py:15
  116.8 2.4 convolution_bitcast_fusion
  119.2 3.6 %copy.26 = f32[16,512,16]{2,0,1:T(8,128)} copy(f32[16,512,16]{1,2,0:T(8,128)S(1)} %convolution_bitcast_fusion) | data formatting | bytes 1048576 | tf_op jit(solution)/shard_map/pqd,cd->pcq/transpose | solution.py:40
  122.8 4.2 %reshape.53 = f32[32,1,4096]{2,1,0:T(1,128)} reshape(f32[512,16,16]{2,1,0:T(8,128)} %bitcast.50) | data formatting | bytes 1048576
  127.0 18.8 %all-to-all-start.1 = ((f32[32,1,4096]{2,1,0:T(1,128)}), f32[32,1,4096]{2,1,0:T(1,128)S(1)}, u32[]{:S(2)}, u32[]{:S(2)}) async-start(f32[32,1,4096]{2,1,0:T(1,128)} %reshape.53), calls=%async_computation.1 | async-start | bytes 1048576 | tf_op jit(solution)/shard_map/all_to_all | solution.py:41
  145.9 2.3 convolution_bitcast_fusion.1
  148.2 3.6 %copy.23 = f32[512,16,16]{1,2,0:T(8,128)} copy(f32[512,16,16]{0,1,2:T(8,128)S(1)} %convolution_bitcast_fusion.1) | data formatting | bytes 1048576 | tf_op jit(solution)/shard_map/pqd,bd->bqp/transpose | solution.py:38
  151.8 4.2 %reshape.55 = f32[32,1,4096]{2,1,0:T(1,128)} reshape(f32[512,16,16]{2,1,0:T(8,128)} %bitcast.51) | data formatting | bytes 1048576
  156.0 17.3 %all-to-all-done.1 = f32[32,1,4096]{2,1,0:T(1,128)S(1)} async-done(((f32[32,1,4096]{2,1,0:T(1,128)}), f32[32,1,4096]{2,1,0:T(1,128)S(1)}, u32[]{:S(2)}, u32[]{:S(2)}) %all-to-all-start.1) | async-done | bytes 524320 | tf_op jit(solution)/shard_map/all_to_all | solution.py:41
  173.3 14.5 %all-to-all-start = ((f32[32,1,4096]{2,1,0:T(1,128)}), f32[32,1,4096]{2,1,0:T(1,128)S(1)}, u32[]{:S(2)}, u32[]{:S(2)}) async-start(f32[32,1,4096]{2,1,0:T(1,128)} %reshape.55), calls=%async_computation | async-start | bytes 1048576 | tf_op jit(solution)/shard_map/all_to_all | solution.py:39
  187.8 0.7 select_reduce_fusion.1
  188.5 0.2 select_reduce_fusion
  188.7 0.7 dynamic-slice_subtract_fusion
  189.5 0.5 broadcast.29
  190.0 1.9 reduce
  192.0 2.8 reshape.54
  194.7 6.6 %copy.28 = f32[16,16,32,16]{3,2,1,0:T(8,128)} copy(f32[16,16,32,16]{3,0,1,2:T(8,128)} %bitcast.52) | data formatting | bytes 1048576 | tf_op jit(solution)/shard_map/all_to_all | solution.py:41
  201.3 4.5 %all_to_all.39 = f32[16,16,512]{2,1,0:T(8,128)S(1)} reshape(f32[16,16,32,16]{3,2,1,0:T(8,128)} %copy.28) | data formatting | bytes 1048576 | tf_op jit(solution)/shard_map/all_to_all | solution.py:41
  205.8 11.1 %all-to-all-done = f32[32,1,4096]{2,1,0:T(1,128)S(1)} async-done(((f32[32,1,4096]{2,1,0:T(1,128)}), f32[32,1,4096]{2,1,0:T(1,128)S(1)}, u32[]{:S(2)}, u32[]{:S(2)}) %all-to-all-start) | async-done | bytes 524320 | tf_op jit(solution)/shard_map/all_to_all | solution.py:39
  216.9 1.9 reduce.1
  218.8 2.8 reshape.56
  221.5 6.4 %copy.25 = f32[16,16,32,16]{3,2,1,0:T(8,128)} copy(f32[16,16,32,16]{1,3,0,2:T(8,128)} %bitcast.53) | data formatting | bytes 1048576 | tf_op jit(solution)/shard_map/all_to_all | solution.py:39
  227.9 4.7 %all_to_all.35 = f32[16,16,512]{2,1,0:T(8,128)S(1)} reshape(f32[16,16,32,16]{3,2,1,0:T(8,128)} %copy.25) | data formatting | bytes 1048576 | tf_op jit(solution)/shard_map/all_to_all | solution.py:39
  232.6 2.3 fusion.6
  234.9 2.8 dot_general.20
  237.7 10.2 %fusion.2 = f32[32,16,512]{2,1,0:T(8,128)S(1)} fusion(f32[32,16,16,16]{1,0,3,2:T(8,128)} %dot_general.20, f32[2,16,16,512]{3,2,1,0:T(8,128)S(1)} %copy-done), kind=kOutput, calls=%fused_computation.2 | convolution fusion | flops 805306368 | bytes 2097152 | tf_op jit(solution)/shard_map/bca,bcd->ad/dot_general | solution.py:56
  247.9 55.7 %all_to_all.46 = f32[32,16,512]{2,1,0:T(8,128)S(1)} all-to-all(f32[32,16,512]{2,1,0:T(8,128)S(1)} %fusion.2), channel_id=1, replica_groups=mesh['vb_0'=4,'vb_1'=8,'vc'=32] {'vb_0','vb_1'}, dimensions={0} | all-to-all | bytes 2097152 | tf_op jit(solution)/shard_map/all_to_all | solution.py:26
  303.8 0.2 copy.30
  304.2 21.6 %all_to_all.47 = f32[32,1,256]{2,1,0:T(1,128)S(1)} all-to-all(f32[32,1,256]{2,1,0:T(1,128)S(1)} %reshape.57), channel_id=1, replica_groups=mesh['vb_0'=4,'vb_1'=8,'vc'=32] {'vc'}, dimensions={0} | all-to-all | bytes 65536 | tf_op jit(solution)/shard_map/all_to_all | solution.py:26
  325.7 0.7 reduce.2
  326.6 0.6 reduce_sum.39
  (19 shorter events, 0.6 us)
Async XLA Ops:
  7.2 109.6 %all-gather.2.cloned.1.call-start = ((), (), s32[]{:S(2)}) async-start(), calls=%async_computation.4 | async-start | bytes 3932160 | tf_op jit(solution)/shard_map/all_gather | solution.py:15
  119.2 26.6 %copy-start = (f32[2,16,16,512]{3,2,1,0:T(8,128)S(1)}, f32[2,16,16,512]{3,2,1,0:T(8,128)}, u32[]{:S(2)}) copy-start(f32[2,16,16,512]{3,2,1,0:T(8,128)} %param.6) | copy-start | bytes 3145732
  127.0 46.2 %all-to-all-start.1 = ((f32[32,1,4096]{2,1,0:T(1,128)}), f32[32,1,4096]{2,1,0:T(1,128)S(1)}, u32[]{:S(2)}, u32[]{:S(2)}) async-start(f32[32,1,4096]{2,1,0:T(1,128)} %reshape.53), calls=%async_computation.1 | async-start | bytes 1048576 | tf_op jit(solution)/shard_map/all_to_all | solution.py:41
  148.2 39.6 %copy-start.4 = (f32[100]{0:T(128)S(1)}, f32[100]{0:T(128)}, u32[]{:S(2)}) copy-start(f32[100]{0:T(128)} %param.8) | copy-start | bytes 1204
  148.2 39.6 %copy-start.5 = (s32[3]{0:T(128)S(1)}, s32[3]{0:T(128)}, u32[]{:S(2)}) copy-start(s32[3]{0:T(128)} %param.10) | copy-start | bytes 40
  148.2 40.3 %copy-start.2 = (f32[512]{0:T(512)S(1)}, f32[512]{0:T(512)}, u32[]{:S(2)}) copy-start(f32[512]{0:T(512)} %param.9) | copy-start | bytes 6148
  148.2 40.3 %copy-start.3 = (s32[512]{0:T(512)S(1)}, s32[512]{0:T(512)}, u32[]{:S(2)}) copy-start(s32[512]{0:T(512)} %param.11) | copy-start | bytes 6148
  173.3 43.6 %all-to-all-start = ((f32[32,1,4096]{2,1,0:T(1,128)}), f32[32,1,4096]{2,1,0:T(1,128)S(1)}, u32[]{:S(2)}, u32[]{:S(2)}) async-start(f32[32,1,4096]{2,1,0:T(1,128)} %reshape.55), calls=%async_computation | async-start | bytes 1048576 | tf_op jit(solution)/shard_map/all_to_all | solution.py:39
  234.9 13.0 %copy-start.1 = (f32[16,16,512]{2,1,0:T(8,128)}, f32[16,16,512]{2,1,0:T(8,128)S(1)}, u32[]{:S(2)}) copy-start(f32[16,16,512]{2,1,0:T(8,128)S(1)} %fusion.6) | copy-start | bytes 1572868
Sparse Core Ops, SparseCore 0:
  60.3 56.4 all-gather.1
where the time goes:
time: 335 us; the launch traced here: 334 us
  blocking collectives  130 us (39%)
  waiting for transfers between devices  84.9 us (25%)
  local copies, waits for them, and re-layouts  47.1 us (14%)
  starting transfers between devices  33.4 us (10%)
  matrix products  17.2 us (5%)
  between operations  14.2 us (4%)
  other arithmetic  6.93 us (2%)
    all_to_all x2, blocking collectives, summed_on_arrival(): lax.all_to_all(pieces, axis, split_axis=0, concat_axis=0, tiled=True)  77.3 us
    all_gather x1, waiting for transfers between devices, gather_axes(): nearer = lax.all_gather(shard, axes[-1], axis=dim, tiled=True)  56.6 us
    all_gather x1, blocking collectives, gather_axes(): nearer = lax.all_gather(shard, axes[-1], axis=dim, tiled=True)  53 us
    all_to_all x1, starting transfers between devices, on_device(): lax.all_to_all(third_local, 'vc', split_axis=1, concat_axis=2, tiled=True)  18.8 us
    all_to_all x1, waiting for transfers between devices, on_device(): lax.all_to_all(third_local, 'vc', split_axis=1, concat_axis=2, tiled=True)  17.3 us
    all_to_all x1, starting transfers between devices, on_device(): lax.all_to_all(second_local, VB, split_axis=0, concat_axis=2, tiled=True)  14.5 us
    unnamed x18, local copies, waits for them, and re-layouts  14.2 us
    all_to_all x3, local copies, waits for them, and re-layouts, on_device(): lax.all_to_all(third_local, 'vc', split_axis=1, concat_axis=2, tiled=True)  11.6 us
  transfers between devices with their start and end apart: 3, of which 3 were waited for; matrix products, arithmetic and copies ran while one was open for 7% of the time, Pallas kernels for 0%

commit v1 on v0

v1 whole, which is shorter than its diff:
```python
import jax
import jax.numpy as jnp
from jax import lax
from jax.experimental import pallas as pl
from jax.experimental.pallas import tpu as pltpu
from jax.sharding import PartitionSpec as P

V = 512
NOCC = 100
MESH = pl.DeviceIdType.MESH
F32 = jnp.float32
BF16 = jnp.bfloat16
NT = (((1,), (1,)), ((), ()))
NN = (((1,), (0,)), ((), ()))


def halves(x):
    high = x.astype(BF16)
    return high, (x - high.astype(F32)).astype(BF16)


def dot3(ah, al, bh, bl, dims):
    def one(a, b):
        return lax.dot_general(a, b, dims, preferred_element_type=F32)

    return one(ah, bh) + (one(ah, bl) + one(al, bh))


def swap_granules(xs, lane):
    xs = list(xs)
    for s in (1, 2, 4):
        upper = (lane & (16 * s)) != 0
        for i in range(8):
            if i & s == 0:
                a, b = xs[i], xs[i + s]
                xs[i] = jnp.where(upper, pltpu.roll(b, 16 * s, 1), a)
                xs[i + s] = jnp.where(upper, b, pltpu.roll(a, 128 - 16 * s, 1))
    return xs


def kernel(
    ints, dbl, eps_occ, eps_virt, triple, order, amp_out, grad_out,
    kf, fi, g_all, kh, kl, ph, plo, ih, il, s2, s3, r2, r3, t2, first, amp, ev, eb,
    part, c0, q0, xr, q1, yr, q2, zr, q3, fr,
    load_sem, zs, zr_sem, ys, yr_sem, xs, xr_sem, cs, cr_sem, as2, ar2, as3, ar3, out_sem,
    ps, pr, gxs, gxr, gys, gyr, gzs, gzr, gfs, gfr,
):
    vb = lax.axis_index("vb")
    vc = lax.axis_index("vc")
    x, z = vb // 8, vb % 8
    h, y, k = vc // 16, (vc // 2) % 8, vc % 2
    other = 1 - k

    def dev(x_=x, z_=z, h_=h, y_=y, k_=k):
        return (x_ * 8 + z_, h_ * 16 + y_ * 2 + k_)

    def send(src, dst, s_sem, r_sem, to):
        pltpu.make_async_remote_copy(
            src_ref=src, dst_ref=dst, send_sem=s_sem, recv_sem=r_sem, device_id=to, device_id_type=MESH
        ).start()

    def drain(ref, sem):
        pltpu.make_async_copy(ref, ref, sem).wait()

    loads = []
    for l in range(4):
        loads.append(pltpu.make_async_copy(ints.at[0, :, pl.ds(128 * l, 128)], kf.at[l], load_sem.at[1]))
        loads.append(pltpu.make_async_copy(ints.at[1, :, pl.ds(128 * l, 128)], fi.at[l], load_sem.at[2]))
    yt, yl = y // 4, y % 4
    mine = z // 4 == k

    @pl.when(mine)
    def _():
        rows = pl.ds(pl.multiple_of(8 * yt, 8), 8)
        cols = pl.ds(pl.multiple_of(128 * yl, 128), 128)
        for m in range(3):
            pltpu.make_async_copy(dbl.at[m, rows, cols], g_all.at[m, vb, yt, yl], load_sem.at[0]).start()

    for copy in loads:
        copy.start()

    barrier = pltpu.get_barrier_semaphore()

    def greet(j, carry):
        pl.semaphore_signal(barrier, inc=1, device_id=((vb + j) % 32, vc), device_id_type=MESH)
        pl.semaphore_signal(barrier, inc=1, device_id=(vb, (vc + j) % 32), device_id_type=MESH)
        return carry

    lax.fori_loop(1, 32, greet, 0)
    for j in range(1, 8):
        pl.semaphore_signal(
            barrier, inc=1, device_id=dev(z_=(z + j) % 8, h_=1 - h), device_id_type=MESH
        )
    pl.semaphore_wait(barrier, 69)

    @pl.when(mine)
    def _():
        drain(g_all.at[0:3, vb, yt, yl], load_sem.at[0])
        for m in (2, 1, 0):
            for j in range(1, 8):
                send(
                    g_all.at[m, vb, yt, yl], g_all.at[m, vb, yt, yl],
                    zs.at[m], zr_sem.at[m], dev(z_=(z + j) % 8),
                )

    drain(kf, load_sem.at[1])
    for l in range(4):
        cols = pl.ds(128 * l, 128)
        high, low = halves(kf[l])
        kh[:, cols] = high
        kl[:, cols] = low
        for c in range(16):
            high, low = halves(kf[l, pl.ds(c, 16, stride=16), :])
            ph[pl.ds(16 * c, 16), cols] = high
            plo[pl.ds(16 * c, 16), cols] = low
    drain(fi, load_sem.at[2])
    for l in range(4):
        cols = pl.ds(128 * l, 128)
        high, low = halves(fi[l])
        ih[:, cols] = high
        il[:, cols] = low

    half = 8 * x + 4 * k
    for m in (2, 1, 0):
        @pl.when(mine)
        def _():
            drain(g_all.at[m, 0, 0, pl.ds(0, 3)], zr_sem.at[m])

        @pl.when(jnp.logical_not(mine))
        def _():
            drain(g_all.at[m, 0, 0], zr_sem.at[m])

        block = g_all.at[m, pl.ds(half, 4), yt, yl]
        for j in range(1, 8):
            send(block, block, ys.at[m], yr_sem.at[m], dev(y_=(y + j) % 8))

    for m in (2, 1, 0):
        drain(g_all.at[0, pl.ds(0, 7), 0], yr_sem.at[m])
        block = g_all.at[m, pl.ds(half, 4)]
        for j in (1, 3, 2):
            send(block, block, xs.at[m], xr_sem.at[m, x], dev(x_=(x + j) % 4))
        send(block, block, cs.at[m], cr_sem.at[m, x], dev(k_=other))

    def rows_of(m, j):
        xg = (x + j) % 4
        if j:
            block = g_all.at[m, pl.ds(8 * xg + 4 * k, 4)]
            drain(block, xr_sem.at[m, xg])
            send(block, block, cs.at[m], cr_sem.at[m, xg], dev(k_=other))
        drain(g_all.at[m, pl.ds(8 * xg + 4 * other, 4)], cr_sem.at[m, xg])
        tiles = g_all.at[m, pl.ds(8 * xg, 8)]
        high, low = halves(
            jnp.concatenate([tiles[:, :, l].reshape(128, 128) for l in range(4)], axis=1)
        )
        return xg, high, low

    for j in (0, 1, 3, 2):
        xg, dh, dl = rows_of(2, j)
        s3[pl.ds(8 * xg, 8)] = dot3(dh, dl, ih[...], il[...], NT).reshape(8, 16, 256)

        def give(i, carry):
            to = 8 * xg + i

            @pl.when(to == vc)
            def _():
                r3[vc] = s3[vc]

            @pl.when(to != vc)
            def _():
                send(s3.at[to], r3.at[vc], as3, ar3, (vb, to))

            return carry

        lax.fori_loop(0, 8, give, 0)

    for j in (0, 1, 3, 2):
        xg, dh, dl = rows_of(1, j)
        s2[pl.ds(8 * xg, 8)] = dot3(dh, dl, ph[...], plo[...], NT).reshape(8, 16, 256)

        def give(i, carry):
            to = 8 * xg + i

            @pl.when(to == vb)
            def _():
                r2[vb] = s2[vb]

            @pl.when(to != vb)
            def _():
                send(s2.at[to], r2.at[vb], as2, ar2, (to, vc))

            return carry

        lax.fori_loop(0, 8, give, 0)

    for j in (0, 1, 3, 2):
        xg, dh, dl = rows_of(0, j)
        first[xg] = dot3(kh[...], kl[...], dh, dl, NT)

    hot = lax.broadcasted_iota(jnp.int32, (V, V), 0) == order[...]
    e_high, e_low = halves(jnp.broadcast_to(eps_virt[...], (8, V)))
    e_rest = (jnp.broadcast_to(eps_virt[...], (8, V)) - e_high.astype(F32) - e_low.astype(F32)).astype(BF16)
    hot = jnp.where(hot, F32(1.0), F32(0.0)).astype(BF16)
    energy = sum(lax.dot_general(e, hot, NN, preferred_element_type=F32) for e in (e_rest, e_low, e_high))[0:1]
    for l in range(4):
        ev[l] = energy[:, 128 * l : 128 * l + 128]
    row = lax.broadcasted_iota(jnp.int32, (256, V), 0)
    col = lax.broadcasted_iota(jnp.int32, (256, V), 1)
    picked = jnp.where(col == 16 * vb + row // 16, energy, F32(0.0))
    b_energy = jnp.sum(picked, axis=1, keepdims=True)
    picked = jnp.where(col == 16 * vc + row % 16, energy, F32(0.0))
    c_energy = jnp.sum(picked, axis=1, keepdims=True)
    occ = eps_occ[0, triple[0, 0]] + eps_occ[0, triple[0, 1]] + eps_occ[0, triple[0, 2]]
    eb[...] = jnp.broadcast_to(occ - b_energy - c_energy, (256, 128))

    drain(s3.at[pl.ds(0, 31)], ar3)
    drain(s2.at[pl.ds(0, 31)], ar2)

    lane = lax.broadcasted_iota(jnp.int32, (8, 128), 1)
    for j in (2, 1, 3, 0):
        g = (x + j) % 4
        for bt in range(2):
            for ch in range(2):
                ws = [r2[8 * g + i, 8 * bt : 8 * bt + 8, 128 * ch : 128 * ch + 128] for i in range(8)]
                for i, w in enumerate(swap_granules(ws, lane)):
                    t2[j, pl.ds(128 * bt + 8 * ch + i, 8, stride=16), :] = w
        for ct in range(2):
            for bh in range(2):
                ws = [r3[8 * g + i, 8 * ct : 8 * ct + 8, 128 * bh : 128 * bh + 128] for i in range(8)]
                for i, w in enumerate(swap_granules(ws, lane)):
                    at = pl.ds((8 * bh + i) * 16 + 8 * ct, 8)
                    first[g, at] = first[g, at] + w
        total = (first[g] + t2[j]) / (eb[...] - ev[g])
        amp[j] = total
        pltpu.make_async_copy(
            amp.at[j], amp_out.at[:, pl.ds(pl.multiple_of(128 * g, 128), 128)], out_sem
        ).start()
        th, tl = halves(total.T)
        part[pl.ds(8 * g, 8)] = dot3(th, tl, kh[...], kl[...], NN).reshape(8, 2, 8, V)
        send(part.at[pl.ds(8 * g, 8), other], c0.at[pl.ds(8 * g, 8)], ps, pr.at[g], dev(k_=other))

    for j in (2, 1, 3, 0):
        g = (x + j) % 4
        block = pl.ds(8 * g, 8)
        drain(c0.at[block], pr.at[g])
        q0[block] = part[block, k] + c0[block]
        if j:
            send(q0.at[block], xr.at[j - 1], gxs, gxr, dev(x_=g))
    drain(xr, gxr)
    q1[...] = (q0[pl.ds(8 * x, 8)] + xr[0]) + (xr[1] + xr[2])
    for j in range(1, 8):
        send(q1.at[(y + j) % 8], yr.at[j - 1], gys, gyr, dev(y_=(y + j) % 8))
    drain(yr, gyr)
    rows = q1[y] + jnp.sum(yr[...], axis=0)
    q2[0] = rows[:, 0:256]
    q2[1] = rows[:, 256:512]
    for hh in range(2):
        here = jnp.logical_and(z == y, h == hh)

        @pl.when(here)
        def _():
            zr[8 * h + z] = q2[hh]

        @pl.when(jnp.logical_not(here))
        def _():
            send(q2.at[hh], zr.at[8 * h + z], gzs.at[hh], gzr, dev(z_=y, h_=hh))

    @pl.when(z == y)
    def _():
        drain(zr.at[pl.ds(0, 15)], gzr)
        total = jnp.sum(zr[...], axis=0)
        q3[0] = total[:, 0:128]
        q3[1] = total[:, 128:256]

        def give(i, carry):
            @pl.when(16 * h + i == vc)
            def _():
                fr[k] = q3[i // 8]

            @pl.when(16 * h + i != vc)
            def _():
                send(q3.at[i // 8], fr.at[k], gfs, gfr.at[k], (vb, 16 * h + i))

            return carry

        lax.fori_loop(0, 16, give, 0)

    for r in range(2):
        @pl.when(jnp.logical_or(z != y, k != r))
        def _():
            drain(fr.at[r], gfr.at[r])

    place = vc % 8
    for r in range(2):
        got = fr[r]
        mine_cols = got[:, 0:16]
        for i in range(1, 8):
            mine_cols = jnp.where(place == i, got[:, 16 * i : 16 * i + 16], mine_cols)
        grad_out[8 * r : 8 * r + 8, :] = mine_cols

    @pl.when(mine)
    def _():
        for m in range(3):
            drain(g_all.at[m, pl.ds(0, 7), 0, 0], zs.at[m])

    for m in range(3):
        drain(g_all.at[0, pl.ds(0, 7), 0], ys.at[m])
        drain(g_all.at[m, pl.ds(0, 12)], xs.at[m])
        drain(g_all.at[m, pl.ds(0, 16)], cs.at[m])
    drain(s3.at[pl.ds(0, 31)], as3)
    drain(s2.at[pl.ds(0, 31)], as2)
    drain(c0, ps)
    drain(xr, gxs)
    drain(yr, gys)
    for hh in range(2):
        @pl.when(jnp.logical_not(jnp.logical_and(z == y, h == hh)))
        def _():
            drain(q2.at[hh], gzs.at[hh])

    @pl.when(z == y)
    def _():
        drain(t2.at[0, pl.ds(0, 120)], gfs)

    drain(amp, out_sem)


def on_device(integrals, doubles, eps_occ, eps_virt, triple, energy_order):
    vmem = pl.BlockSpec(memory_space=pltpu.VMEM)
    smem = pl.BlockSpec(memory_space=pltpu.SMEM)
    anyw = pl.BlockSpec(memory_space=pl.ANY)
    dma = pltpu.SemaphoreType.DMA
    f = lambda *s: pltpu.VMEM(s, F32)
    b = lambda *s: pltpu.VMEM(s, BF16)
    amp, grad = pl.pallas_call(
        kernel,
        out_shape=(jax.ShapeDtypeStruct((256, V), F32), jax.ShapeDtypeStruct((16, 16), F32)),
        in_specs=[anyw, anyw, smem, vmem, smem, vmem],
        out_specs=(anyw, vmem),
        scratch_shapes=[
            f(4, 256, 128), f(4, 256, 128), f(3, 32, 2, 4, 8, 128),
            b(256, V), b(256, V), b(256, V), b(256, V), b(256, V), b(256, V),
            f(32, 16, 256), f(32, 16, 256), f(32, 16, 256), f(32, 16, 256),
            f(4, 256, 128), f(4, 256, 128), f(4, 256, 128), f(4, 1, 128), f(256, 128),
            f(32, 2, 8, V), f(32, 8, V), f(32, 8, V), f(3, 8, 8, V), f(8, 8, V), f(7, 8, V),
            f(2, 8, 256), f(16, 8, 256), f(2, 8, 128), f(2, 8, 128),
            dma((3,)), dma((3,)), dma((3,)), dma((3,)), dma((3,)), dma((3,)), dma((3, 4)), dma((3,)), dma((3, 4)),
            dma, dma, dma, dma, dma,
            dma, dma((4,)), dma, dma, dma, dma, dma((2,)), dma, dma, dma((2,)),
        ],
        compiler_params=pltpu.CompilerParams(
            collective_id=0, has_side_effects=True, vmem_limit_bytes=48 * 1024 * 1024
        ),
    )(
        integrals.reshape(2, 256, V),
        doubles,
        eps_occ.reshape(1, NOCC),
        eps_virt.reshape(1, V),
        triple.reshape(1, 3),
        energy_order.reshape(1, V),
    )
    return amp.reshape(16, 16, V), grad


def solution(mesh):
    return jax.shard_map(
        on_device,
        mesh=mesh,
        in_specs=(P(None, "vb", "vc", None), P(None, "vb", None), P(), P(), P(), P()),
        out_specs=(P("vb", "vc", None), P("vb", "vc")),
        check_vma=False,
    )
```

time: 335 us -> 124 us (0.37)
  blocking collectives: 130 us -> 0 us
  Pallas kernels: 0 us -> 119 us
  waiting for transfers between devices: 84.9 us -> 0 us
  local copies, waits for them, and re-layouts: 47.1 us -> 4.18 us
  starting transfers between devices: 33.4 us -> 0 us
  matrix products: 17.2 us -> 0 us
  between operations: 14.2 us -> 0.68 us
  other arithmetic: 6.93 us -> 0 us
    pallas_call x0 -> x1, Pallas kernels: none -> 119 us  [on_device(): pl.pallas_call(kernel, out_shape=(jax.ShapeDtypeStruct((256, V), F32), ja...]
    all_to_all x2 -> x0, blocking collectives: 77.3 us -> none  [summed_on_arrival(): lax.all_to_all(pieces, axis, split_axis=0, concat_axis=0, tiled=True)]
    all_gather x1 -> x0, waiting for transfers between devices: 56.6 us -> none  [gather_axes(): nearer = lax.all_gather(shard, axes[-1], axis=dim, tiled=True)]
    all_gather x1 -> x0, blocking collectives: 53 us -> none  [gather_axes(): nearer = lax.all_gather(shard, axes[-1], axis=dim, tiled=True)]
    all_to_all x2 -> x0, starting transfers between devices: 33.3 us -> none  [the longest x1 18.8 us: on_device(): lax.all_to_all(third_local, 'vc', split_axis=1, concat_axis=2, tiled=True)]
    all_to_all x2 -> x0, waiting for transfers between devices: 28.3 us -> none  [the longest x1 17.3 us: on_device(): lax.all_to_all(third_local, 'vc', split_axis=1, concat_axis=2, tiled=True)]
    all_to_all x5 -> x0, local copies, waits for them, and re-layouts: 22.7 us -> none  [the longest x3 11.6 us: on_device(): lax.all_to_all(third_local, 'vc', split_axis=1, concat_axis=2, tiled=True)]
    dot_general x4 -> x0, matrix products: 17.2 us -> none  [the longest x1 10.2 us: on_device(): jnp.einsum('bca,bcd->ad', amplitudes, k_block, precision=highest)]
  transfers between devices with their start and end apart: 3 -> 0, of which waited for: 3 -> 0; matrix products, arithmetic and copies ran while one was open for 7% -> 0% of each run, Pallas kernels for 0% -> 0%
where the time goes in v1:
time: 124 us; the launch traced here: 123 us
  Pallas kernels  119 us (96%)
  local copies, waits for them, and re-layouts  4.18 us (3%)
    pallas_call x1, Pallas kernels, on_device(): pl.pallas_call(kernel, out_shape=(jax.ShapeDtypeStruct((256, V), F32), ja...  119 us
    unnamed x14, local copies, waits for them, and re-layouts  4.18 us

profile of v1, /device:TPU:1, one launch (start us, length us, event | category | flops | bytes accessed | tf_op | source)
XLA Modules:
  0.0 123.4 jit_solution(12384898220525524558)
XLA Ops:
  0.6 0.0 copy-start.3
  0.6 0.0 copy-start.2
  0.7 0.0 copy-start.4
  0.7 0.0 copy-start.5
  0.7 0.6 copy-done.3
  1.3 0.0 copy-done.2
  1.3 0.0 copy-done.4
  1.3 0.0 copy-done.5
  1.3 0.0 copy-start
  1.3 1.2 copy-done
  2.6 0.0 copy-start.1
  2.6 0.9 copy-done.1
  3.5 118.6 %shard_map.77 = (f32[256,512]{1,0:T(8,128)S(1)}, f32[16,16]{1,0:T(8,128)S(1)}) custom-call(f32[2,256,512]{2,1,0:T(8,128)S(1)} %bitcast.6, f32[3,16,512]{2,1,0:T(8,128)S(1)} %copy-done.1, f32[1,100]{1,0:T(1,128)S(1)} %bitcast.10, f32[1,512]{1,0:T(1,128)S(1)} %bitcast.8, s32[1,3]{1,0:T(1,128)S(1)} %bitcast.11, s32[1,512]{1,0:T(1,128)S(1)} %bitcast.9), custom_call_target="tpu_custom_call" | custom-call | tf_op jit(solution)/shard_map/pallas_call | solution.py:333
  122.1 0.8 copy.10
  122.8 0.6 copy.11
Async XLA Ops:
  0.6 0.7 copy-start.3
  0.6 0.7 copy-start.2
  0.7 0.7 copy-start.4
  0.7 0.7 copy-start.5
  1.3 1.2 copy-start
  2.6 0.9 copy-start.1

commit v2 on v1

--- a/solution.py
+++ b/solution.py
@@ -39,7 +39,8 @@
 
 
 def kernel(
-    ints, dbl, eps_occ, eps_virt, triple, order, amp_out, grad_out,
+    ints, dbl, eps_occ_in, eps_virt_in, triple_in, order_in, amp_out, grad_out,
+    eps_occ, eps_virt, triple, order,
     kf, fi, g_all, kh, kl, ph, plo, ih, il, s2, s3, r2, r3, t2, first, amp, ev, eb,
     part, c0, q0, xr, q1, yr, q2, zr, q3, fr,
     load_sem, zs, zr_sem, ys, yr_sem, xs, xr_sem, cs, cr_sem, as2, ar2, as3, ar3, out_sem,
@@ -76,21 +77,21 @@
         for m in range(3):
             pltpu.make_async_copy(dbl.at[m, rows, cols], g_all.at[m, vb, yt, yl], load_sem.at[0]).start()
 
-    for copy in loads:
-        copy.start()
+    small = [(eps_occ_in, eps_occ), (eps_virt_in, eps_virt), (triple_in, triple), (order_in, order)]
 
     barrier = pltpu.get_barrier_semaphore()
 
-    def greet(j, carry):
-        pl.semaphore_signal(barrier, inc=1, device_id=((vb + j) % 32, vc), device_id_type=MESH)
-        pl.semaphore_signal(barrier, inc=1, device_id=(vb, (vc + j) % 32), device_id_type=MESH)
-        return carry
-
-    lax.fori_loop(1, 32, greet, 0)
+    for j in range(1, 32):
+        pl.semaphore_signal(barrier, inc=1, device_id=(lax.rem(vb + j, 32), vc), device_id_type=MESH)
+        pl.semaphore_signal(barrier, inc=1, device_id=(vb, lax.rem(vc + j, 32)), device_id_type=MESH)
     for j in range(1, 8):
         pl.semaphore_signal(
             barrier, inc=1, device_id=dev(z_=(z + j) % 8, h_=1 - h), device_id_type=MESH
         )
+    for copy in loads:
+        copy.start()
+    for i, (src, dst) in enumerate(small):
+        pltpu.make_async_copy(src, dst, load_sem.at[3 + i]).start()
     pl.semaphore_wait(barrier, 69)
 
     @pl.when(mine)
@@ -98,9 +99,11 @@
         drain(g_all.at[0:3, vb, yt, yl], load_sem.at[0])
         for m in (2, 1, 0):
             for j in range(1, 8):
+                to = (z + j) % 8
+                near = jnp.abs(to - z) <= 4
                 send(
                     g_all.at[m, vb, yt, yl], g_all.at[m, vb, yt, yl],
-                    zs.at[m], zr_sem.at[m], dev(z_=(z + j) % 8),
+                    zs.at[m], zr_sem.at[m], dev(z_=to, h_=jnp.where(near, h, 1 - h)),
                 )
 
     drain(kf, load_sem.at[1])
@@ -134,19 +137,21 @@
         for j in range(1, 8):
             send(block, block, ys.at[m], yr_sem.at[m], dev(y_=(y + j) % 8))
 
-    for m in (2, 1, 0):
+    def spread(m):
         drain(g_all.at[0, pl.ds(0, 7), 0], yr_sem.at[m])
         block = g_all.at[m, pl.ds(half, 4)]
+        send(block, block, cs.at[m], cr_sem.at[m, x], dev(k_=other))
         for j in (1, 3, 2):
             send(block, block, xs.at[m], xr_sem.at[m, x], dev(x_=(x + j) % 4))
-        send(block, block, cs.at[m], cr_sem.at[m, x], dev(k_=other))
+
+    def forward(m, j):
+        xg = (x + j) % 4
+        block = g_all.at[m, pl.ds(8 * xg + 4 * k, 4)]
+        drain(block, xr_sem.at[m, xg])
+        send(block, block, cs.at[m], cr_sem.at[m, xg], dev(k_=other))
 
     def rows_of(m, j):
         xg = (x + j) % 4
-        if j:
-            block = g_all.at[m, pl.ds(8 * xg + 4 * k, 4)]
-            drain(block, xr_sem.at[m, xg])
-            send(block, block, cs.at[m], cr_sem.at[m, xg], dev(k_=other))
         drain(g_all.at[m, pl.ds(8 * xg + 4 * other, 4)], cr_sem.at[m, xg])
         tiles = g_all.at[m, pl.ds(8 * xg, 8)]
         high, low = halves(
@@ -154,12 +159,12 @@
         )
         return xg, high, low
 
-    for j in (0, 1, 3, 2):
+    def third(j):
         xg, dh, dl = rows_of(2, j)
         s3[pl.ds(8 * xg, 8)] = dot3(dh, dl, ih[...], il[...], NT).reshape(8, 16, 256)
 
         def give(i, carry):
-            to = 8 * xg + i
+            to = 8 * xg + (i + vc) % 8
 
             @pl.when(to == vc)
             def _():
@@ -167,18 +172,18 @@
 
             @pl.when(to != vc)
             def _():
-                send(s3.at[to], r3.at[vc], as3, ar3, (vb, to))
+                send(s3.at[to], r3.at[vc], as3, ar3.at[vc // 8], (vb, to))
 
             return carry
 
         lax.fori_loop(0, 8, give, 0)
 
-    for j in (0, 1, 3, 2):
+    def second(j):
         xg, dh, dl = rows_of(1, j)
         s2[pl.ds(8 * xg, 8)] = dot3(dh, dl, ph[...], plo[...], NT).reshape(8, 16, 256)
 
         def give(i, carry):
-            to = 8 * xg + i
+            to = 8 * xg + (i + vb + 4) % 8
 
             @pl.when(to == vb)
             def _():
@@ -186,16 +191,41 @@
 
             @pl.when(to != vb)
             def _():
-                send(s2.at[to], r2.at[vb], as2, ar2, (to, vc))
+                send(s2.at[to], r2.at[vb], as2, ar2.at[x], (to, vc))
 
             return carry
 
         lax.fori_loop(0, 8, give, 0)
 
-    for j in (0, 1, 3, 2):
+    def first_term(j):
         xg, dh, dl = rows_of(0, j)
         first[xg] = dot3(kh[...], kl[...], dh, dl, NT)
 
+    spread(2)
+    spread(1)
+    third(0)
+    spread(0)
+    forward(2, 1)
+    forward(2, 3)
+    third(1)
+    third(3)
+    forward(2, 2)
+    forward(1, 1)
+    third(2)
+    forward(1, 3)
+    second(1)
+    forward(1, 2)
+    second(3)
+    forward(0, 1)
+    forward(0, 3)
+    second(2)
+    forward(0, 2)
+    second(0)
+    for j in (0, 1, 3, 2):
+        first_term(j)
+
+    for i, (_, dst) in enumerate(small):
+        drain(dst, load_sem.at[3 + i])
     hot = lax.broadcasted_iota(jnp.int32, (V, V), 0) == order[...]
     e_high, e_low = halves(jnp.broadcast_to(eps_virt[...], (8, V)))
     e_rest = (jnp.broadcast_to(eps_virt[...], (8, V)) - e_high.astype(F32) - e_low.astype(F32)).astype(BF16)
@@ -209,42 +239,63 @@
     b_energy = jnp.sum(picked, axis=1, keepdims=True)
     picked = jnp.where(col == 16 * vc + row % 16, energy, F32(0.0))
     c_energy = jnp.sum(picked, axis=1, keepdims=True)
-    occ = eps_occ[0, triple[0, 0]] + eps_occ[0, triple[0, 1]] + eps_occ[0, triple[0, 2]]
+    place = lax.broadcasted_iota(jnp.int32, (1, NOCC), 1)
+    occ = sum(
+        jnp.sum(jnp.where(place == triple[:, i : i + 1], eps_occ[...], F32(0.0)), axis=1, keepdims=True)
+        for i in range(3)
+    )
     eb[...] = jnp.broadcast_to(occ - b_energy - c_energy, (256, 128))
 
-    drain(s3.at[pl.ds(0, 31)], ar3)
-    drain(s2.at[pl.ds(0, 31)], ar2)
-
     lane = lax.broadcasted_iota(jnp.int32, (8, 128), 1)
-    for j in (2, 1, 3, 0):
+
+    def group(j):
         g = (x + j) % 4
-        for bt in range(2):
-            for ch in range(2):
-                ws = [r2[8 * g + i, 8 * bt : 8 * bt + 8, 128 * ch : 128 * ch + 128] for i in range(8)]
-                for i, w in enumerate(swap_granules(ws, lane)):
-                    t2[j, pl.ds(128 * bt + 8 * ch + i, 8, stride=16), :] = w
+
+        @pl.when(g == vc // 8)
+        def _():
+            drain(s3.at[pl.ds(0, 7)], ar3.at[g])
+
+        @pl.when(g != vc // 8)
+        def _():
+            drain(s3.at[pl.ds(0, 8)], ar3.at[g])
+
         for ct in range(2):
             for bh in range(2):
                 ws = [r3[8 * g + i, 8 * ct : 8 * ct + 8, 128 * bh : 128 * bh + 128] for i in range(8)]
                 for i, w in enumerate(swap_granules(ws, lane)):
                     at = pl.ds((8 * bh + i) * 16 + 8 * ct, 8)
                     first[g, at] = first[g, at] + w
+        drain(s2.at[pl.ds(0, 8 if j else 7)], ar2.at[g])
+        for bt in range(2):
+            for ch in range(2):
+                ws = [r2[8 * g + i, 8 * bt : 8 * bt + 8, 128 * ch : 128 * ch + 128] for i in range(8)]
+                for i, w in enumerate(swap_granules(ws, lane)):
+                    t2[j, pl.ds(128 * bt + 8 * ch + i, 8, stride=16), :] = w
         total = (first[g] + t2[j]) / (eb[...] - ev[g])
         amp[j] = total
+        th, tl = halves(total.T)
+        part[pl.ds(8 * g, 8)] = dot3(th, tl, kh[...], kl[...], NN).reshape(8, 2, 8, V)
+        send(part.at[pl.ds(8 * g, 8), other], c0.at[pl.ds(8 * g, 8)], ps, pr.at[g], dev(k_=other))
         pltpu.make_async_copy(
             amp.at[j], amp_out.at[:, pl.ds(pl.multiple_of(128 * g, 128), 128)], out_sem
         ).start()
-        th, tl = halves(total.T)
-        part[pl.ds(8 * g, 8)] = dot3(th, tl, kh[...], kl[...], NN).reshape(8, 2, 8, V)
-        send(part.at[pl.ds(8 * g, 8), other], c0.at[pl.ds(8 * g, 8)], ps, pr.at[g], dev(k_=other))
-
-    for j in (2, 1, 3, 0):
+
+    def over_cores(j):
         g = (x + j) % 4
         block = pl.ds(8 * g, 8)
         drain(c0.at[block], pr.at[g])
         q0[block] = part[block, k] + c0[block]
         if j:
             send(q0.at[block], xr.at[j - 1], gxs, gxr, dev(x_=g))
+
+    group(3)
+    group(1)
+    over_cores(3)
+    group(2)
+    over_cores(1)
+    over_cores(2)
+    group(0)
+    over_cores(0)
     drain(xr, gxr)
     q1[...] = (q0[pl.ds(8 * x, 8)] + xr[0]) + (xr[1] + xr[2])
     for j in range(1, 8):
@@ -325,7 +376,6 @@
 
 def on_device(integrals, doubles, eps_occ, eps_virt, triple, energy_order):
     vmem = pl.BlockSpec(memory_space=pltpu.VMEM)
-    smem = pl.BlockSpec(memory_space=pltpu.SMEM)
     anyw = pl.BlockSpec(memory_space=pl.ANY)
     dma = pltpu.SemaphoreType.DMA
     f = lambda *s: pltpu.VMEM(s, F32)
@@ -333,21 +383,22 @@
     amp, grad = pl.pallas_call(
         kernel,
         out_shape=(jax.ShapeDtypeStruct((256, V), F32), jax.ShapeDtypeStruct((16, 16), F32)),
-        in_specs=[anyw, anyw, smem, vmem, smem, vmem],
+        in_specs=[anyw] * 6,
         out_specs=(anyw, vmem),
         scratch_shapes=[
+            f(1, NOCC), f(1, V), pltpu.VMEM((1, 3), jnp.int32), pltpu.VMEM((1, V), jnp.int32),
             f(4, 256, 128), f(4, 256, 128), f(3, 32, 2, 4, 8, 128),
             b(256, V), b(256, V), b(256, V), b(256, V), b(256, V), b(256, V),
             f(32, 16, 256), f(32, 16, 256), f(32, 16, 256), f(32, 16, 256),
             f(4, 256, 128), f(4, 256, 128), f(4, 256, 128), f(4, 1, 128), f(256, 128),
             f(32, 2, 8, V), f(32, 8, V), f(32, 8, V), f(3, 8, 8, V), f(8, 8, V), f(7, 8, V),
             f(2, 8, 256), f(16, 8, 256), f(2, 8, 128), f(2, 8, 128),
-            dma((3,)), dma((3,)), dma((3,)), dma((3,)), dma((3,)), dma((3,)), dma((3, 4)), dma((3,)), dma((3, 4)),
-            dma, dma, dma, dma, dma,
+            dma((7,)), dma((3,)), dma((3,)), dma((3,)), dma((3,)), dma((3,)), dma((3, 4)), dma((3,)), dma((3, 4)),
+            dma, dma((4,)), dma, dma((4,)), dma,
             dma, dma((4,)), dma, dma, dma, dma, dma((2,)), dma, dma, dma((2,)),
         ],
         compiler_params=pltpu.CompilerParams(
-            collective_id=0, has_side_effects=True, vmem_limit_bytes=48 * 1024 * 1024
+            collective_id=0, has_side_effects=True, vmem_limit_bytes=60 * 1024 * 1024
         ),
     )(
         integrals.reshape(2, 256, V),

time: 124 us -> 119 us (0.960)
  Pallas kernels: 119 us -> 116 us
  local copies, waits for them, and re-layouts: 4.18 us -> 2.49 us
    pallas_call x1, Pallas kernels: 119 us -> 116 us  [on_device(): pl.pallas_call(kernel, out_shape=(jax.ShapeDtypeStruct((256, V), F32), ja...]
    unnamed x14 -> x4, local copies, waits for them, and re-layouts: 4.18 us -> 2.49 us
where the time goes in v2:
time: 119 us
  Pallas kernels  116 us (97%)
  local copies, waits for them, and re-layouts  2.49 us (2%)
    pallas_call x1, Pallas kernels, on_device(): pl.pallas_call(kernel, out_shape=(jax.ShapeDtypeStruct((256, V), F32), ja...  116 us
    unnamed x4, local copies, waits for them, and re-layouts  2.49 us

profile of v2, /device:TPU:1, one launch (start us, length us, event | category | flops | bytes accessed | tf_op | source)
XLA Modules:
  0.0 118.8 jit_solution(9456648452491647428)
XLA Ops:
  0.6 115.6 %shard_map.77 = (f32[256,512]{1,0:T(8,128)}, f32[16,16]{1,0:T(8,128)}) custom-call(f32[2,256,512]{2,1,0:T(8,128)} %bitcast.6, f32[3,16,512]{2,1,0:T(8,128)} %dbl.1, f32[1,100]{1,0:T(1,128)} %bitcast.10, f32[1,512]{1,0:T(1,128)} %bitcast.8, s32[1,3]{1,0:T(1,128)} %bitcast.11, s32[1,512]{1,0:T(1,128)} %bitcast.9), custom_call_target="tpu_custom_call" | custom-call | tf_op jit(solution)/shard_map/pallas_call | solution.py:383
  116.3 0.0 copy-start
  116.3 1.9 %copy.10 = f32[16,16,512]{2,1,0:T(8,128)} copy(f32[16,16,512]{2,1,0:T(8,128)} %bitcast.7) | data formatting | bytes 1048576
  118.2 0.0 copy-done
  118.2 0.6 copy.11
Async XLA Ops:
  116.3 1.9 %copy-start = (f32[16,16]{1,0:T(8,128)S(1)}, f32[16,16]{1,0:T(8,128)}, u32[]{:S(2)}) copy-start(f32[16,16]{1,0:T(8,128)} %get-tuple-element.9) | copy-start | bytes 3076

commit v3 on v2

--- a/solution.py
+++ b/solution.py
@@ -42,9 +42,9 @@
     ints, dbl, eps_occ_in, eps_virt_in, triple_in, order_in, amp_out, grad_out,
     eps_occ, eps_virt, triple, order,
     kf, fi, g_all, kh, kl, ph, plo, ih, il, s2, s3, r2, r3, t2, first, amp, ev, eb,
-    part, c0, q0, xr, q1, yr, q2, zr, q3, fr,
+    part, c0, q0, xr, q1, q2, zr, fr,
     load_sem, zs, zr_sem, ys, yr_sem, xs, xr_sem, cs, cr_sem, as2, ar2, as3, ar3, out_sem,
-    ps, pr, gxs, gxr, gys, gyr, gzs, gzr, gfs, gfr,
+    ps, pr, gxs, gxr, gzs, gzr, gfs, gfr, far_sem,
 ):
     vb = lax.axis_index("vb")
     vc = lax.axis_index("vc")
@@ -81,18 +81,30 @@
 
     barrier = pltpu.get_barrier_semaphore()
 
+    far = [(vb, 16 * (1 - h) + i) for i in range(16)]
+    far += [dev(z_=lax.rem(z + j, 8), h_=1 - h) for j in range(1, 8)]
     for j in range(1, 32):
         pl.semaphore_signal(barrier, inc=1, device_id=(lax.rem(vb + j, 32), vc), device_id_type=MESH)
-        pl.semaphore_signal(barrier, inc=1, device_id=(vb, lax.rem(vc + j, 32)), device_id_type=MESH)
-    for j in range(1, 8):
-        pl.semaphore_signal(
-            barrier, inc=1, device_id=dev(z_=(z + j) % 8, h_=1 - h), device_id_type=MESH
-        )
+    for j in range(1, 16):
+        to = 16 * h + lax.rem(vc % 16 + j, 16)
+        pl.semaphore_signal(barrier, inc=1, device_id=(vb, to), device_id_type=MESH)
+
+    @pl.when(h == 0)
+    def _():
+        for to in far:
+            pl.semaphore_signal(barrier, inc=1, device_id=to, device_id_type=MESH)
+
     for copy in loads:
         copy.start()
     for i, (src, dst) in enumerate(small):
         pltpu.make_async_copy(src, dst, load_sem.at[3 + i]).start()
-    pl.semaphore_wait(barrier, 69)
+    pl.semaphore_wait(barrier, 46 + 23 * h)
+
+    @pl.when(h == 1)
+    def _():
+        for to in far:
+            pl.semaphore_signal(far_sem, inc=1, device_id=to, device_id_type=MESH)
+
 
     @pl.when(mine)
     def _():
@@ -100,10 +112,9 @@
         for m in (2, 1, 0):
             for j in range(1, 8):
                 to = (z + j) % 8
-                near = jnp.abs(to - z) <= 4
                 send(
                     g_all.at[m, vb, yt, yl], g_all.at[m, vb, yt, yl],
-                    zs.at[m], zr_sem.at[m], dev(z_=to, h_=jnp.where(near, h, 1 - h)),
+                    zs.at[m], zr_sem.at[m], dev(z_=to),
                 )
 
     drain(kf, load_sem.at[1])
@@ -203,6 +214,11 @@
 
     spread(2)
     spread(1)
+
+    @pl.when(h == 0)
+    def _():
+        pl.semaphore_wait(far_sem, 23)
+
     third(0)
     spread(0)
     forward(2, 1)
@@ -297,52 +313,25 @@
     group(0)
     over_cores(0)
     drain(xr, gxr)
-    q1[...] = (q0[pl.ds(8 * x, 8)] + xr[0]) + (xr[1] + xr[2])
-    for j in range(1, 8):
-        send(q1.at[(y + j) % 8], yr.at[j - 1], gys, gyr, dev(y_=(y + j) % 8))
-    drain(yr, gyr)
-    rows = q1[y] + jnp.sum(yr[...], axis=0)
-    q2[0] = rows[:, 0:256]
-    q2[1] = rows[:, 256:512]
-    for hh in range(2):
-        here = jnp.logical_and(z == y, h == hh)
-
-        @pl.when(here)
-        def _():
-            zr[8 * h + z] = q2[hh]
-
-        @pl.when(jnp.logical_not(here))
-        def _():
-            send(q2.at[hh], zr.at[8 * h + z], gzs.at[hh], gzr, dev(z_=y, h_=hh))
-
-    @pl.when(z == y)
-    def _():
-        drain(zr.at[pl.ds(0, 15)], gzr)
-        total = jnp.sum(zr[...], axis=0)
-        q3[0] = total[:, 0:128]
-        q3[1] = total[:, 128:256]
-
-        def give(i, carry):
-            @pl.when(16 * h + i == vc)
-            def _():
-                fr[k] = q3[i // 8]
-
-            @pl.when(16 * h + i != vc)
-            def _():
-                send(q3.at[i // 8], fr.at[k], gfs, gfr.at[k], (vb, 16 * h + i))
-
-            return carry
-
-        lax.fori_loop(0, 16, give, 0)
-
-    for r in range(2):
-        @pl.when(jnp.logical_or(z != y, k != r))
-        def _():
-            drain(fr.at[r], gfr.at[r])
-
+    rows = (q0[pl.ds(8 * x, 8)] + xr[0]) + (xr[1] + xr[2])
+    q1[0] = rows[:, :, 0:256]
+    q1[1] = rows[:, :, 256:512]
+    for o in (8, 7, 9, 6, 10, 5, 11, 4, 12, 3, 13, 2, 14, 1, 15):
+        to = lax.rem(8 * h + z + o, 16)
+        send(q1.at[to // 8, to % 8], zr.at[8 * h + z], gzs, gzr, dev(z_=to % 8, h_=to // 8))
+    zr[8 * h + z] = q1[h, z]
+    drain(zr.at[pl.ds(0, 15)], gzr)
+    total = jnp.sum(zr[...], axis=0)
+    q2[0] = total[:, 0:128]
+    q2[1] = total[:, 128:256]
+    for o in (8, 9, 7, 6, 10, 5, 11, 4, 12, 3, 13, 2, 14, 1, 15):
+        to = lax.rem(vc % 16 + o, 16)
+        send(q2.at[to // 8], fr.at[vc % 16], gfs, gfr, (vb, 16 * h + to))
+    fr[vc % 16] = q2[(vc % 16) // 8]
+    drain(fr.at[pl.ds(0, 15)], gfr)
     place = vc % 8
     for r in range(2):
-        got = fr[r]
+        got = sum(fr[2 * i + r] for i in range(8))
         mine_cols = got[:, 0:16]
         for i in range(1, 8):
             mine_cols = jnp.where(place == i, got[:, 16 * i : 16 * i + 16], mine_cols)
@@ -361,16 +350,8 @@
     drain(s2.at[pl.ds(0, 31)], as2)
     drain(c0, ps)
     drain(xr, gxs)
-    drain(yr, gys)
-    for hh in range(2):
-        @pl.when(jnp.logical_not(jnp.logical_and(z == y, h == hh)))
-        def _():
-            drain(q2.at[hh], gzs.at[hh])
-
-    @pl.when(z == y)
-    def _():
-        drain(t2.at[0, pl.ds(0, 120)], gfs)
-
+    drain(zr.at[pl.ds(0, 15)], gzs)
+    drain(fr.at[pl.ds(0, 15)], gfs)
     drain(amp, out_sem)
 
 
@@ -391,11 +372,12 @@
             b(256, V), b(256, V), b(256, V), b(256, V), b(256, V), b(256, V),
             f(32, 16, 256), f(32, 16, 256), f(32, 16, 256), f(32, 16, 256),
             f(4, 256, 128), f(4, 256, 128), f(4, 256, 128), f(4, 1, 128), f(256, 128),
-            f(32, 2, 8, V), f(32, 8, V), f(32, 8, V), f(3, 8, 8, V), f(8, 8, V), f(7, 8, V),
-            f(2, 8, 256), f(16, 8, 256), f(2, 8, 128), f(2, 8, 128),
+            f(32, 2, 8, V), f(32, 8, V), f(32, 8, V), f(3, 8, 8, V), f(2, 8, 8, 256),
+            f(2, 8, 128), f(16, 8, 256), f(16, 8, 128),
             dma((7,)), dma((3,)), dma((3,)), dma((3,)), dma((3,)), dma((3,)), dma((3, 4)), dma((3,)), dma((3, 4)),
             dma, dma((4,)), dma, dma((4,)), dma,
-            dma, dma((4,)), dma, dma, dma, dma, dma((2,)), dma, dma, dma((2,)),
+            dma, dma((4,)), dma, dma, dma, dma, dma, dma,
+            pltpu.SemaphoreType.REGULAR,
         ],
         compiler_params=pltpu.CompilerParams(
             collective_id=0, has_side_effects=True, vmem_limit_bytes=60 * 1024 * 1024

time: 119 us -> 114 us (0.958)
  Pallas kernels: 116 us -> 110 us
    pallas_call x1, Pallas kernels: 116 us -> 110 us  [on_device(): pl.pallas_call(kernel, out_shape=(jax.ShapeDtypeStruct((256, V), F32), ja...]
where the time goes in v3:
time: 114 us; the launch traced here: 113 us
  Pallas kernels  110 us (96%)
  local copies, waits for them, and re-layouts  2.49 us (2%)
    pallas_call x1, Pallas kernels, on_device(): pl.pallas_call(kernel, out_shape=(jax.ShapeDtypeStruct((256, V), F32), ja...  110 us
    unnamed x4, local copies, waits for them, and re-layouts  2.49 us

profile of v3, /device:TPU:1, one launch (start us, length us, event | category | flops | bytes accessed | tf_op | source)
XLA Modules:
  0.0 113.5 jit_solution(13575854913544398152)
XLA Ops:
  0.6 110.4 %shard_map.77 = (f32[256,512]{1,0:T(8,128)}, f32[16,16]{1,0:T(8,128)}) custom-call(f32[2,256,512]{2,1,0:T(8,128)} %bitcast.6, f32[3,16,512]{2,1,0:T(8,128)} %dbl.1, f32[1,100]{1,0:T(1,128)} %bitcast.10, f32[1,512]{1,0:T(1,128)} %bitcast.8, s32[1,3]{1,0:T(1,128)} %bitcast.11, s32[1,512]{1,0:T(1,128)} %bitcast.9), custom_call_target="tpu_custom_call" | custom-call | tf_op jit(solution)/shard_map/pallas_call | solution.py:364
  111.0 0.0 copy-start
  111.0 1.9 %copy.10 = f32[16,16,512]{2,1,0:T(8,128)} copy(f32[16,16,512]{2,1,0:T(8,128)} %bitcast.7) | data formatting | bytes 1048576
  112.9 0.0 copy-done
  112.9 0.6 copy.11
Async XLA Ops:
  111.0 1.9 %copy-start = (f32[16,16]{1,0:T(8,128)S(1)}, f32[16,16]{1,0:T(8,128)}, u32[]{:S(2)}) copy-start(f32[16,16]{1,0:T(8,128)} %get-tuple-element.9) | copy-start | bytes 3076
